TPU v7x, 8 devices: a whole 2x2x1 slice. The times are simulated.
8 devices in a mesh: data: 2 (over z, y), seq: 4 (over x, core).
Axes of the slice: x: 2, y: 2, z: 1, core: 2. Of those that a mesh axis runs over, the one named last changes fastest.
Arguments:
- act_in: bfloat16 [8, 1024, 1024], P('data', 'seq'), parts along dimension 0
- ln1_scale: float32 [1024], replicated
- ln1_bias: float32 [1024], replicated
- w_in: bfloat16 [1024, 6144], replicated
- b_in: float32 [6144], replicated
- ln2_scale: float32 [3072], replicated
- ln2_bias: float32 [3072], replicated
- w_spatial: bfloat16 [1024, 1024], replicated
- b_spatial: float32 [1024], replicated
- causal_mask: int32 [1024, 1024], replicated
- w_out: bfloat16 [3072, 1024], replicated
- b_out: float32 [1024], replicated
Outputs:
- output: bfloat16 [8, 1024, 1024], P('data', 'seq'), parts along dimension 0
There are 2 independent parts. A program takes and returns all parts, laid end to end along the dimension named above; an argument that names none is the same for every part.
All inputs are finite; a program needn't handle non-finite values.
Results may differ from a plain program's by a relative error of at most 0.0115622.
Values are sent between devices in bfloat16 or wider.
A program may use at most 1 GiB of HBM per device.

v0:
```python
import jax
import jax.numpy as jnp
from jax import lax
from jax.sharding import PartitionSpec as P

LN_EPS = 1e-6


def layer_norm(features, ln_gain, ln_shift):
    mean_val = jnp.mean(features, axis=-1, keepdims=True)
    centered = features - mean_val
    var_val = jnp.mean(centered * centered, axis=-1, keepdims=True)
    return centered * lax.rsqrt(var_val + LN_EPS) * ln_gain + ln_shift


def solution(mesh):
    row_spec = P('data', 'seq', None)
    replicated = P()

    def local_block(act_in, ln1_scale, ln1_bias, w_in, b_in, ln2_scale, ln2_bias, w_spatial, b_spatial, causal_mask, w_out, b_out):
        gate_dim = w_out.shape[0]
        normed = layer_norm(act_in.astype(jnp.float32), ln1_scale, ln1_bias).astype(jnp.bfloat16)
        hidden = jax.nn.gelu(jnp.einsum('bsd,df->bsf', normed, w_in, preferred_element_type=jnp.float32) + b_in, approximate=True).astype(jnp.bfloat16)
        gate_half = hidden[:, :, :gate_dim]
        value_norm = layer_norm(hidden[:, :, gate_dim:].astype(jnp.float32), ln2_scale, ln2_bias).astype(jnp.bfloat16)
        value_cols = lax.all_to_all(value_norm, 'seq', 2, 1, tiled=True)
        w_masked = jnp.where(causal_mask > 0, w_spatial, jnp.zeros_like(w_spatial))
        spatial_cols = (jnp.einsum('ij,bjc->bic', w_masked, value_cols, preferred_element_type=jnp.float32) + b_spatial[None, :, None]).astype(jnp.bfloat16)
        spatial_rows = lax.all_to_all(spatial_cols, 'seq', 1, 2, tiled=True)
        gated_act = (gate_half.astype(jnp.float32) * spatial_rows.astype(jnp.float32)).astype(jnp.bfloat16)
        projected = jnp.einsum('bsc,cd->bsd', gated_act, w_out, preferred_element_type=jnp.float32) + b_out
        return (act_in.astype(jnp.float32) + projected).astype(jnp.bfloat16)

    return jax.shard_map(local_block, mesh=mesh, in_specs=(row_spec,) + (replicated,) * 11, out_specs=row_spec, check_vma=False)
```

profile of v0, /device:TPU:0, one launch (start us, length us, event | category | flops | bytes accessed | tf_op | source)
XLA Modules:
  0.0 291.2 jit_solution(2329042409557086412)
XLA Ops:
  0.0 1.9 convert_reduce_fusion.1
  1.9 2.3 fusion.21
  4.2 26.8 %fusion.7 = bf16[4,256,6144]{2,1,0:T(8,128)(2,1)} fusion(bf16[1024,6144]{1,0:T(8,128)(2,1)} %param.15, f32[6144]{0:T(1024)} %param.16, bf16[4,256,1024]{2,1,0:T(8,128)(2,1)} %param.12, f32[1024]{0:T(1024)} %param.14, f32[1024]{0:T(1024)} %param.13, f32[4,256]{1,0:T(4,128)S(1)} %add_rsqrt_fusion.1, f32[4,256]{1,0:T(4,128)S(1)} %broadcast_multiply_fusion.1), kind=kOutput, calls=%fused_computation.8 | convolution fusion | flops 12954107904 | bytes 27303936 | tf_op jit(solution)/shard_map/bsd,df->bsf/dot_general | solution.py:23
  31.0 0.0 copy-start
  31.0 0.0 copy-start.2
  31.0 0.0 copy-start.3
  31.0 3.8 %convert_reduce_fusion = f32[4,256]{1,0:T(4,128)S(1)} fusion(bf16[4,256,6144]{2,1,0:T(8,128)(2,1)} %fusion.7), kind=kLoop, calls=%fused_computation.10 | loop fusion | flops 6290432 | bytes 6295552 | tf_op jit(solution)/shard_map/reduce_sum | solution.py:10
  34.9 5.3 %fusion.10 = f32[4,256]{1,0:T(4,128)S(1)} fusion(f32[4,256]{1,0:T(4,128)S(1)} %broadcast_multiply_fusion, bf16[4,256,6144]{2,1,0:T(8,128)(2,1)} %fusion.7), kind=kLoop, calls=%fused_computation.13 | loop fusion | flops 12581888 | bytes 6299648 | tf_op jit(solution)/shard_map/reduce_sum | solution.py:12
  40.2 0.0 copy-done
  40.3 0.0 copy-done.2
  40.3 0.0 copy-done.3
  40.3 5.0 %fusion.13 = bf16[4,256,3072]{2,1,0:T(8,128)(2,1)} fusion(f32[3072]{0:T(1024)S(1)} %copy-done.2, f32[3072]{0:T(1024)S(1)} %copy-done.3, f32[4,256]{1,0:T(4,128)S(1)} %add_rsqrt_fusion, f32[4,256]{1,0:T(4,128)S(1)} %broadcast_multiply_fusion, bf16[4,256,6144]{2,1,0:T(8,128)(2,1)S(1)} %copy-done), kind=kLoop, calls=%fused_computation.16 | loop fusion | flops 18874368 | bytes 12615680 | tf_op jit(solution)/shard_map/convert_element_type | solution.py:25
  45.3 10.6 %copy.15 = bf16[4,256,3072]{1,0,2:T(4,128)(2,1)} copy(bf16[4,256,3072]{2,1,0:T(8,128)(2,1)} %fusion.13) | data formatting | bytes 12582912 | tf_op jit(solution)/shard_map/convert_element_type | solution.py:25
  55.9 75.6 %all_to_all.27 = bf16[4,256,3072]{1,0,2:T(4,128)(2,1)S(1)} all-to-all(bf16[4,256,3072]{1,0,2:T(4,128)(2,1)} %copy.15), channel_id=1, replica_groups=mesh['data'=2,'seq'=4] {'seq'}, dimensions={2} | all-to-all | bytes 12582912 | tf_op jit(solution)/shard_map/all_to_all | solution.py:26
  131.4 7.4 %copy.22 = bf16[4,256,4,768]{1,2,3,0:T(4,128)(2,1)} copy(bf16[4,256,4,768]{1,0,3,2:T(4,128)(2,1)S(1)} %bitcast.26) | data formatting | bytes 12582912 | tf_op jit(solution)/shard_map/all_to_all | solution.py:26
  138.9 0.0 copy-start.4
  138.9 0.0 copy-start.5
  138.9 11.2 %all_to_all.23 = bf16[4,1024,768]{1,2,0:T(8,128)(2,1)} reshape(bf16[4,4,256,768]{2,1,3,0:T(4,128)(2,1)} %bitcast.27) | data formatting | bytes 12582912 | tf_op jit(solution)/shard_map/all_to_all | solution.py:26
  150.1 0.0 copy-done.4
  150.1 0.0 copy-done.5
  150.1 12.1 %fusion.15 = bf16[4,1024,768]{1,2,0:T(8,128)(2,1)} fusion(f32[1024]{0:T(1024)S(1)} %copy-done.5, bf16[4,1024,768]{1,2,0:T(8,128)(2,1)} %all_to_all.23, bf16[1024,1024]{1,0:T(8,128)(2,1)S(1)} %copy-done.4, s32[1024,1024]{1,0:T(8,128)} %param.21), kind=kOutput, calls=%fused_computation.21 | convolution fusion | flops 6450839552 | bytes 18878464 | tf_op jit(solution)/shard_map/ij,bjc->bic/dot_general | solution.py:28
  162.2 10.7 %copy.17 = bf16[4,1024,768]{2,0,1:T(4,128)(2,1)} copy(bf16[4,1024,768]{1,2,0:T(8,128)(2,1)} %fusion.15) | data formatting | bytes 12582912 | tf_op jit(solution)/shard_map/convert_element_type | solution.py:28
  172.9 77.0 %all_to_all.28 = bf16[4,1024,768]{2,0,1:T(4,128)(2,1)} all-to-all(bf16[4,1024,768]{2,0,1:T(4,128)(2,1)} %copy.17), channel_id=1, replica_groups=mesh['data'=2,'seq'=4] {'seq'}, dimensions={1} | all-to-all | bytes 12582912 | tf_op jit(solution)/shard_map/all_to_all | solution.py:29
  249.9 12.1 %copy.21 = f32[4,4,256,768]{3,1,2,0:T(4,128)} copy(bf16[4,4,256,768]{3,0,2,1:T(4,128)(2,1)} %bitcast.28) | data formatting | bytes 18874368 | tf_op jit(solution)/shard_map/convert_element_type | solution.py:30
  262.1 0.0 copy-start.1
  262.1 0.0 copy-start.6
  262.1 15.8 %reshape.35 = f32[4,256,3072]{2,1,0:T(8,128)} reshape(f32[4,256,4,768]{3,2,1,0:T(4,128)} %bitcast.25) | data formatting | bytes 25165824 | tf_op jit(solution)/shard_map/convert_element_type | solution.py:30
  277.9 0.0 copy-done.1
  277.9 0.0 copy-done.6
  277.9 13.4 %fusion.25 = bf16[4,256,1024]{2,1,0:T(8,128)(2,1)} fusion(bf16[4,256,1024]{2,1,0:T(8,128)(2,1)S(1)} %copy-done.1, bf16[3072,1024]{1,0:T(8,128)(2,1)} %param.22, f32[4,256,3072]{2,1,0:T(8,128)} %reshape.35, bf16[4,256,6144]{2,1,0:T(8,128)(2,1)} %fusion.7, f32[1024]{0:T(1024)S(1)} %copy-done.6), kind=kOutput, calls=%fused_computation.35 | convolution fusion | flops 6456082432 | bytes 29364224 | tf_op jit(solution)/shard_map/bsc,cd->bsd/dot_general | solution.py:31
  (4 shorter events, 0.0 us)
Async XLA Ops:
  31.0 9.2 %copy-start = (bf16[4,256,6144]{2,1,0:T(8,128)(2,1)S(1)}, bf16[4,256,6144]{2,1,0:T(8,128)(2,1)}, u32[]{:S(2)}) copy-start(bf16[4,256,6144]{2,1,0:T(8,128)(2,1)} %fusion.7) | copy-start | bytes 37748740
  31.0 9.2 %copy-start.2 = (f32[3072]{0:T(1024)S(1)}, f32[3072]{0:T(1024)}, u32[]{:S(2)}) copy-start(f32[3072]{0:T(1024)} %param.18) | copy-start | bytes 36868
  31.0 9.2 %copy-start.3 = (f32[3072]{0:T(1024)S(1)}, f32[3072]{0:T(1024)}, u32[]{:S(2)}) copy-start(f32[3072]{0:T(1024)} %param.17) | copy-start | bytes 36868
  138.9 11.2 %copy-start.4 = (bf16[1024,1024]{1,0:T(8,128)(2,1)S(1)}, bf16[1024,1024]{1,0:T(8,128)(2,1)}, u32[]{:S(2)}) copy-start(bf16[1024,1024]{1,0:T(8,128)(2,1)} %param.19) | copy-start | bytes 6291460
  138.9 11.2 %copy-start.5 = (f32[1024]{0:T(1024)S(1)}, f32[1024]{0:T(1024)}, u32[]{:S(2)}) copy-start(f32[1024]{0:T(1024)} %param.20) | copy-start | bytes 12292
  262.1 15.8 %copy-start.1 = (bf16[4,256,1024]{2,1,0:T(8,128)(2,1)S(1)}, bf16[4,256,1024]{2,1,0:T(8,128)(2,1)}, u32[]{:S(2)}) copy-start(bf16[4,256,1024]{2,1,0:T(8,128)(2,1)} %param.12) | copy-start | bytes 6291460
  262.1 15.8 %copy-start.6 = (f32[1024]{0:T(1024)S(1)}, f32[1024]{0:T(1024)}, u32[]{:S(2)}) copy-start(f32[1024]{0:T(1024)} %param.23) | copy-start | bytes 12292
where the time goes:
time: 293 us; the launch traced here: 291 us
  blocking collectives  153 us (52%)
  local copies, waits for them, and re-layouts  67.9 us (23%)
  matrix products  52.3 us (18%)
  other arithmetic  18.5 us (6%)
    all_to_all x1, blocking collectives, local_block(): spatial_rows = lax.all_to_all(spatial_cols, 'seq', 1, 2, tiled=True)  77 us
    all_to_all x1, blocking collectives, local_block(): value_cols = lax.all_to_all(value_norm, 'seq', 2, 1, tiled=True)  75.6 us
    convert_element_type x2, local copies, waits for them, and re-layouts, local_block(): spatial_rows.astype(jnp.float32)  27.9 us
    dot_general x1, matrix products, local_block(): jnp.einsum('bsd,df->bsf', normed, w_in, preferred_element_type=jnp.float32)  26.8 us
    all_to_all x2, local copies, waits for them, and re-layouts, local_block(): value_cols = lax.all_to_all(value_norm, 'seq', 2, 1, tiled=True)  18.6 us
    dot_general x1, matrix products, local_block(): jnp.einsum('bsc,cd->bsd', gated_act, w_out, preferred_element_type=jnp.fl...  13.4 us
    dot_general x1, matrix products, local_block(): jnp.einsum('ij,bjc->bic', w_masked, value_cols, preferred_element_type=jn...  12.1 us
    convert_element_type x1, local copies, waits for them, and re-layouts, local_block(): (jnp.einsum('ij,bjc->bic', w_masked, value_cols, preferred_element_type=j...  10.7 us

commit v1 on v0

v1 whole, which is shorter than its diff:
```python
import functools

import jax
import jax.numpy as jnp
from jax import lax
from jax.experimental import pallas as pl
from jax.experimental.pallas import tpu as pltpu
from jax.sharding import PartitionSpec as P

LN_EPS = 1e-6
GELU_A = 0.7978845608028654
GELU_B = GELU_A * 0.044715
COLS = 512
MESH = pl.DeviceIdType.MESH
F32 = jnp.float32
BF16 = jnp.bfloat16


def gelu(a):
    half = 0.5 * a
    return half + half * jnp.tanh(a * (GELU_A + GELU_B * (a * a)))


def layer_norm(x, gain, shift):
    width = x.shape[-1]
    mean = jnp.sum(x, axis=-1, keepdims=True) * (1.0 / width)
    centered = x - mean
    var = jnp.sum(centered * centered, axis=-1, keepdims=True) * (1.0 / width)
    return centered * lax.rsqrt(var + LN_EPS) * gain + shift


def body(n, act, ln1s, ln1b, w_in, b_in, ln2s, ln2b, w_sp, b_sp, mask, w_out, b_out, out,
         xbuf, wi, wo, ws, mk, vn, g, u, q, ybuf, bias,
         xs_sem, xr_sem, ys_sem, yr_sem, wi_sem, wo_sem, ws_sem, mk_sem):
    me = lax.axis_index("seq")
    chip, core = me // 2, lax.rem(me, 2)
    partner = chip * 2 + 1 - core
    far = (1 - chip) * 2
    rows, width = act.shape[1], act.shape[2]
    gate = w_out.shape[0]
    n_cols = gate // COLS

    def wi_copy(c):
        cols = pl.ds(c * COLS, COLS)
        return pltpu.make_async_copy(w_in.at[:, cols], wi.at[:, cols], wi_sem.at[c])

    def ws_copy(i):
        where = (pl.ds(i * rows, rows), pl.ds(0, (i + 1) * rows))
        return pltpu.make_async_copy(w_sp.at[where], ws.at[where], ws_sem.at[i])

    def mk_copy(i):
        where = (pl.ds(i * rows, rows), pl.ds(0, (i + 1) * rows))
        return pltpu.make_async_copy(mask.at[where], mk.at[where], mk_sem.at[i])

    def own_x():
        return pltpu.make_async_copy(act.at[me], xbuf.at[me], xr_sem.at[me])

    def wo_copy():
        return pltpu.make_async_copy(w_out, wo, wo_sem)

    def x_send(dest):
        return pltpu.make_async_remote_copy(
            src_ref=act.at[dest], dst_ref=xbuf.at[me], send_sem=xs_sem.at[dest], recv_sem=xr_sem.at[me],
            device_id={"seq": dest}, device_id_type=MESH)

    def x_recv(block):
        return pltpu.make_async_remote_copy(
            src_ref=act.at[block], dst_ref=xbuf.at[block], send_sem=xs_sem.at[block], recv_sem=xr_sem.at[block],
            device_id={"seq": block}, device_id_type=MESH)

    def y_send(block):
        return pltpu.make_async_remote_copy(
            src_ref=ybuf.at[block], dst_ref=out.at[me], send_sem=ys_sem.at[block], recv_sem=yr_sem.at[me],
            device_id={"seq": block}, device_id_type=MESH)

    def y_recv(block):
        return pltpu.make_async_remote_copy(
            src_ref=ybuf.at[block], dst_ref=out.at[block], send_sem=ys_sem.at[block], recv_sem=yr_sem.at[block],
            device_id={"seq": block}, device_id_type=MESH)

    def y_own():
        return pltpu.make_async_copy(ybuf.at[me], out.at[me], yr_sem.at[me])

    barrier = pltpu.get_barrier_semaphore()
    for k in range(1, n):
        pl.semaphore_signal(barrier, inc=1, device_id={"seq": lax.rem(me + k, n)}, device_id_type=MESH)
    own_x().start()
    order = list(range(n_cols, 2 * n_cols)) + list(range(n_cols))
    for c in order:
        wi_copy(c).start()
    pl.semaphore_wait(barrier, n - 1)
    for dest in (far, partner, far + 1):
        x_send(dest).start()
    for i in range(n):
        ws_copy(i).start()
        mk_copy(i).start()
    wo_copy().start()

    for i in range(n):
        at = pl.ds(i * rows, rows)
        bias[at, :] = jnp.broadcast_to(b_sp[:, at], (128, rows)).T

    def stage_a(t, first):
        block = lax.rem(2 * chip + t, n)
        at = pl.multiple_of(block * rows, rows)

        @pl.when(block == me)
        def _():
            own_x().wait()

        @pl.when(block != me)
        def _():
            x_recv(block).wait_recv()

        step1 = 64
        for r in range(rows // step1):
            part = pl.ds(r * step1, step1)
            u[part, :] = layer_norm(xbuf[block, part, :].astype(F32), ln1s[...], ln1b[...]).astype(BF16)

        def chunk(c):
            if first:
                wi_copy(c).wait()
            cols = pl.ds(c * COLS, COLS)
            acc = jnp.dot(u[...], wi[:, cols], preferred_element_type=F32)
            return gelu(acc + b_in[:, cols]).astype(BF16)

        for c in range(n_cols):
            vn[pl.ds(at, rows), pl.ds(c * COLS, COLS)] = chunk(n_cols + c)
        for c in range(n_cols):
            g[pl.ds(at, rows), pl.ds(c * COLS, COLS)] = chunk(c)
        step2 = 16

        def norm(r, carry):
            part = pl.ds(pl.multiple_of(at + r * step2, step2), step2)
            vn[part, :] = layer_norm(vn[part, :].astype(F32), ln2s[...], ln2b[...]).astype(BF16)
            return carry

        lax.fori_loop(0, rows // step2, norm, 0)

    def stage_b(i):
        at = pl.ds(i * rows, rows)
        depth = (i + 1) * rows
        ws_copy(i).wait()
        mk_copy(i).wait()
        for r in range(i + 1):
            cols = pl.ds(r * rows, rows)
            ws[at, cols] = jnp.where(mk[at, cols] > 0, ws[at, cols].astype(F32), 0.0).astype(BF16)
        if i == 0:
            wo_copy().wait()
        bias_cols = jnp.concatenate([bias[at, :]] * (COLS // 128), axis=1)
        for c in range(n_cols):
            cols = pl.ds(c * COLS, COLS)
            s = jnp.dot(ws[at, :depth], vn[:depth, cols], preferred_element_type=F32) + bias_cols
            q[:, cols] = (g[at, cols].astype(F32) * s.astype(BF16).astype(F32)).astype(BF16)
        for c in range(width // COLS):
            cols = pl.ds(c * COLS, COLS)
            y = jnp.dot(q[...], wo[:, cols], preferred_element_type=F32) + b_out[:, cols]
            ybuf[i, :, cols] = (xbuf[i, :, cols].astype(F32) + y).astype(BF16)

        @pl.when(me == i)
        def _():
            y_own().start()

        @pl.when(me != i)
        def _():
            y_send(i).start()

    stage_a(0, True)

    def outer(k, carry):
        def upto(k):
            return (1 - chip) * (2 + k // 2 + k // 3) + chip * (3 + (k + 2) // 3)

        def one(t, c):
            stage_a(t, False)
            return c

        low = jnp.where(k == 0, 1, upto(k - 1)) if not isinstance(k, int) else (1 if k == 0 else upto(k - 1))
        lax.fori_loop(low, upto(k), one, 0)
        for i in range(n):
            pl.when(k == i)(functools.partial(stage_b, i))
        return carry

    lax.fori_loop(0, n, outer, 0)

    for k in range(1, n):
        peer = lax.rem(me + k, n)
        x_send(peer).wait_send()
        y_send(peer).wait_send()
        y_recv(peer).wait_recv()
    y_own().wait()


def solution(mesh):
    n = mesh.shape["seq"]
    row_spec = P("data", "seq", None)

    def local_block(act_in, ln1_scale, ln1_bias, w_in, b_in, ln2_scale, ln2_bias, w_spatial, b_spatial, causal_mask, w_out, b_out):
        batch, rows, width = act_in.shape
        length = batch * 0 + n * rows
        gate = w_out.shape[0]
        hbm = pl.BlockSpec(memory_space=pl.ANY)
        vmem = pl.BlockSpec(memory_space=pltpu.VMEM)

        def row(v):
            return v.reshape(1, -1)

        return pl.pallas_call(
            functools.partial(body, n),
            out_shape=jax.ShapeDtypeStruct(act_in.shape, act_in.dtype),
            in_specs=[hbm, vmem, vmem, hbm, vmem, vmem, vmem, hbm, vmem, hbm, hbm, vmem],
            out_specs=hbm,
            scratch_shapes=[
                pltpu.VMEM((n, rows, width), BF16),
                pltpu.VMEM((width, 2 * gate), BF16),
                pltpu.VMEM((gate, width), BF16),
                pltpu.VMEM((length, length), BF16),
                pltpu.VMEM((length, length), jnp.int32),
                pltpu.VMEM((length, gate), BF16),
                pltpu.VMEM((length, gate), BF16),
                pltpu.VMEM((rows, width), BF16),
                pltpu.VMEM((rows, gate), BF16),
                pltpu.VMEM((n, rows, width), BF16),
                pltpu.VMEM((length, 128), F32),
                pltpu.SemaphoreType.DMA((n,)),
                pltpu.SemaphoreType.DMA((n,)),
                pltpu.SemaphoreType.DMA((n,)),
                pltpu.SemaphoreType.DMA((n,)),
                pltpu.SemaphoreType.DMA((2 * gate // COLS,)),
                pltpu.SemaphoreType.DMA,
                pltpu.SemaphoreType.DMA((n,)),
                pltpu.SemaphoreType.DMA((n,)),
            ],
            compiler_params=pltpu.CompilerParams(
                collective_id=0, has_side_effects=True, vmem_limit_bytes=60 * 1024 * 1024),
            name="gmlp",
        )(act_in, row(ln1_scale), row(ln1_bias), w_in, row(b_in), row(ln2_scale), row(ln2_bias),
          w_spatial, row(b_spatial), causal_mask, w_out, row(b_out))

    return jax.shard_map(local_block, mesh=mesh, in_specs=(row_spec,) + (P(),) * 11, out_specs=row_spec, check_vma=False)
```

time: 293 us -> 70.8 us (0.24)
  blocking collectives: 153 us -> 0 us
  Pallas kernels: 0 us -> 67.5 us
  local copies, waits for them, and re-layouts: 67.9 us -> 3.08 us
  matrix products: 52.3 us -> 0 us
  other arithmetic: 18.5 us -> 0 us
    all_to_all x2 -> x0, blocking collectives: 153 us -> none  [the longest x1 77 us: local_block(): spatial_rows = lax.all_to_all(spatial_cols, 'seq', 1, 2, tiled=True)]
    pallas_call x0 -> x1, Pallas kernels: none -> 67.5 us  [local_block(): pl.pallas_call(functools.partial(body, n), out_shape=jax.ShapeDtypeStruct...]
    dot_general x3 -> x0, matrix products: 52.3 us -> none  [the longest x1 26.8 us: local_block(): jnp.einsum('bsd,df->bsf', normed, w_in, preferred_element_type=jnp.float32)]
    convert_element_type x4 -> x0, local copies, waits for them, and re-layouts: 49.2 us -> none  [the longest x2 27.9 us: local_block(): spatial_rows.astype(jnp.float32)]
    all_to_all x2 -> x0, local copies, waits for them, and re-layouts: 18.6 us -> none  [local_block(): value_cols = lax.all_to_all(value_norm, 'seq', 2, 1, tiled=True)]
    reduce_sum x4 -> x0, other arithmetic: 13.4 us -> none  [the longest x2 7.63 us: layer_norm(): var_val = jnp.mean(centered * centered, axis=-1, keepdims=True)]
    convert_element_type x1 -> x0, other arithmetic: 5.04 us -> none  [local_block(): layer_norm(hidden[:, :, gate_dim:].astype(jnp.float32), ln2_scale, ln2_bias)]
    unnamed x14 -> x1, local copies, waits for them, and re-layouts: 0.03 us -> 3.08 us
where the time goes in v1:
time: 70.8 us; the launch traced here: 70.6 us
  Pallas kernels  67.5 us (95%)
  local copies, waits for them, and re-layouts  3.08 us (4%)
    pallas_call x1, Pallas kernels, local_block(): pl.pallas_call(functools.partial(body, n), out_shape=jax.ShapeDtypeStruct...  67.5 us
    unnamed x1, local copies, waits for them, and re-layouts  3.08 us

profile of v1, /device:TPU:0, one launch (start us, length us, event | category | flops | bytes accessed | tf_op | source)
XLA Modules:
  0.0 70.6 jit_solution(11522648879601421376)
XLA Ops:
  0.0 67.5 %gmlp.1 = bf16[4,256,1024]{2,1,0:T(8,128)(2,1)} custom-call(bf16[4,256,1024]{2,1,0:T(8,128)(2,1)} %act.1, f32[1,1024]{1,0:T(1,128)} %bitcast.10, f32[1,1024]{1,0:T(1,128)} %bitcast.11, bf16[1024,6144]{1,0:T(8,128)(2,1)} %w_in.1, f32[1,6144]{1,0:T(1,128)} %bitcast.7, f32[1,3072]{1,0:T(1,128)} %bitcast.8, f32[1,3072]{1,0:T(1,128)} %bitcast.9, ...), custom_call_target="tpu_custom_call" | custom-call | tf_op jit(solution)/shard_map/gmlp/pallas_call | solution.py:208
  67.5 3.1 %copy.14 = bf16[4,256,1024]{2,1,0:T(8,128)(2,1)} copy(bf16[4,256,1024]{2,1,0:T(8,128)(2,1)} %gmlp.1) | data formatting | bytes 4194304

commit v2 on v1

--- a/solution.py
+++ b/solution.py
@@ -30,7 +30,7 @@
 
 
 def body(n, act, ln1s, ln1b, w_in, b_in, ln2s, ln2b, w_sp, b_sp, mask, w_out, b_out, out,
-         xbuf, wi, wo, ws, mk, vn, g, u, q, ybuf, bias,
+         xbuf, wi, wo, ws, mk, h, u, q, ybuf, bias, acc0, acc1,
          xs_sem, xr_sem, ys_sem, yr_sem, wi_sem, wo_sem, ws_sem, mk_sem):
     me = lax.axis_index("seq")
     chip, core = me // 2, lax.rem(me, 2)
@@ -40,17 +40,20 @@
     gate = w_out.shape[0]
     n_cols = gate // COLS
 
+    def cols_of(c):
+        return pl.ds(pl.multiple_of(c * COLS, COLS), COLS)
+
+    def rows_of(i):
+        return pl.ds(pl.multiple_of(i * rows, rows), rows)
+
     def wi_copy(c):
-        cols = pl.ds(c * COLS, COLS)
-        return pltpu.make_async_copy(w_in.at[:, cols], wi.at[:, cols], wi_sem.at[c])
+        return pltpu.make_async_copy(w_in.at[:, cols_of(c)], wi.at[:, cols_of(c)], wi_sem.at[c])
 
     def ws_copy(i):
-        where = (pl.ds(i * rows, rows), pl.ds(0, (i + 1) * rows))
-        return pltpu.make_async_copy(w_sp.at[where], ws.at[where], ws_sem.at[i])
+        return pltpu.make_async_copy(w_sp.at[rows_of(i)], ws.at[rows_of(i)], ws_sem.at[i])
 
     def mk_copy(i):
-        where = (pl.ds(i * rows, rows), pl.ds(0, (i + 1) * rows))
-        return pltpu.make_async_copy(mask.at[where], mk.at[where], mk_sem.at[i])
+        return pltpu.make_async_copy(mask.at[rows_of(i)], mk.at[rows_of(i)], mk_sem.at[i])
 
     def own_x():
         return pltpu.make_async_copy(act.at[me], xbuf.at[me], xr_sem.at[me])
@@ -85,8 +88,7 @@
     for k in range(1, n):
         pl.semaphore_signal(barrier, inc=1, device_id={"seq": lax.rem(me + k, n)}, device_id_type=MESH)
     own_x().start()
-    order = list(range(n_cols, 2 * n_cols)) + list(range(n_cols))
-    for c in order:
+    for c in range(2 * n_cols):
         wi_copy(c).start()
     pl.semaphore_wait(barrier, n - 1)
     for dest in (far, partner, far + 1):
@@ -96,13 +98,9 @@
         mk_copy(i).start()
     wo_copy().start()
 
-    for i in range(n):
-        at = pl.ds(i * rows, rows)
-        bias[at, :] = jnp.broadcast_to(b_sp[:, at], (128, rows)).T
-
-    def stage_a(t, first):
+    def stage_a(t):
         block = lax.rem(2 * chip + t, n)
-        at = pl.multiple_of(block * rows, rows)
+        at = rows_of(block)
 
         @pl.when(block == me)
         def _():
@@ -112,50 +110,93 @@
         def _():
             x_recv(block).wait_recv()
 
-        step1 = 64
-        for r in range(rows // step1):
-            part = pl.ds(r * step1, step1)
+        step1 = 32
+
+        def norm1(r, carry):
+            part = pl.ds(pl.multiple_of(r * step1, step1), step1)
             u[part, :] = layer_norm(xbuf[block, part, :].astype(F32), ln1s[...], ln1b[...]).astype(BF16)
-
-        def chunk(c):
-            if first:
+            return carry
+
+        lax.fori_loop(0, rows // step1, norm1, 0)
+
+        def dot(c):
+            return jnp.dot(u[...], wi[:, cols_of(c)], preferred_element_type=F32)
+
+        def finish(acc, c):
+            h[at, cols_of(c)] = gelu(acc[...] + b_in[:, cols_of(c)]).astype(BF16)
+
+        def pair(p, carry):
+            c = 2 * p
+
+            @pl.when(t == 0)
+            def _():
                 wi_copy(c).wait()
-            cols = pl.ds(c * COLS, COLS)
-            acc = jnp.dot(u[...], wi[:, cols], preferred_element_type=F32)
-            return gelu(acc + b_in[:, cols]).astype(BF16)
-
-        for c in range(n_cols):
-            vn[pl.ds(at, rows), pl.ds(c * COLS, COLS)] = chunk(n_cols + c)
-        for c in range(n_cols):
-            g[pl.ds(at, rows), pl.ds(c * COLS, COLS)] = chunk(c)
+                wi_copy(c + 1).wait()
+
+            acc0[...] = dot(c)
+            finish(acc1, lax.rem(c + 2 * n_cols - 1, 2 * n_cols))
+            acc1[...] = dot(c + 1)
+            finish(acc0, c)
+            return carry
+
+        lax.fori_loop(0, n_cols, pair, 0)
+        finish(acc1, 2 * n_cols - 1)
         step2 = 16
 
-        def norm(r, carry):
-            part = pl.ds(pl.multiple_of(at + r * step2, step2), step2)
-            vn[part, :] = layer_norm(vn[part, :].astype(F32), ln2s[...], ln2b[...]).astype(BF16)
-            return carry
-
-        lax.fori_loop(0, rows // step2, norm, 0)
+        def norm2(r, carry):
+            part = (pl.ds(pl.multiple_of(block * rows + r * step2, step2), step2), pl.ds(gate, gate))
+            h[part] = layer_norm(h[part].astype(F32), ln2s[...], ln2b[...]).astype(BF16)
+            return carry
+
+        lax.fori_loop(0, rows // step2, norm2, 0)
 
     def stage_b(i):
-        at = pl.ds(i * rows, rows)
-        depth = (i + 1) * rows
+        at = rows_of(i)
+        bias[...] = jnp.broadcast_to(b_sp[:, at], (128, rows)).T
         ws_copy(i).wait()
         mk_copy(i).wait()
-        for r in range(i + 1):
-            cols = pl.ds(r * rows, rows)
-            ws[at, cols] = jnp.where(mk[at, cols] > 0, ws[at, cols].astype(F32), 0.0).astype(BF16)
-        if i == 0:
+        step = 32
+
+        def select(r, carry):
+            part = pl.ds(pl.multiple_of(i * rows + r * step, step), step)
+            ws[part, :] = jnp.where(mk[part, :] > 0, ws[part, :].astype(F32), 0.0).astype(BF16)
+            return carry
+
+        lax.fori_loop(0, rows // step, select, 0)
+
+        @pl.when(i == 0)
+        def _():
             wo_copy().wait()
-        bias_cols = jnp.concatenate([bias[at, :]] * (COLS // 128), axis=1)
-        for c in range(n_cols):
-            cols = pl.ds(c * COLS, COLS)
-            s = jnp.dot(ws[at, :depth], vn[:depth, cols], preferred_element_type=F32) + bias_cols
-            q[:, cols] = (g[at, cols].astype(F32) * s.astype(BF16).astype(F32)).astype(BF16)
-        for c in range(width // COLS):
-            cols = pl.ds(c * COLS, COLS)
+
+        def finish(acc, c):
+            s = acc[...] + jnp.concatenate([bias[...]] * (COLS // 128), axis=1)
+            q[:, cols_of(c)] = (h[at, cols_of(c)].astype(F32) * s.astype(BF16).astype(F32)).astype(BF16)
+
+        def spatial(depth):
+            def dot(c):
+                return jnp.dot(ws[at, :depth], h[:depth, cols_of(n_cols + c)], preferred_element_type=F32)
+
+            def pair(p, carry):
+                c = 2 * p
+                acc0[...] = dot(c)
+                finish(acc1, lax.rem(c + n_cols - 1, n_cols))
+                acc1[...] = dot(c + 1)
+                finish(acc0, c)
+                return carry
+
+            lax.fori_loop(0, n_cols // 2, pair, 0)
+
+        for k in range(n):
+            pl.when(i == k)(functools.partial(spatial, (k + 1) * rows))
+        finish(acc1, n_cols - 1)
+
+        def project(c, carry):
+            cols = cols_of(c)
             y = jnp.dot(q[...], wo[:, cols], preferred_element_type=F32) + b_out[:, cols]
             ybuf[i, :, cols] = (xbuf[i, :, cols].astype(F32) + y).astype(BF16)
+            return carry
+
+        lax.fori_loop(0, width // COLS, project, 0)
 
         @pl.when(me == i)
         def _():
@@ -164,21 +205,17 @@
         @pl.when(me != i)
         def _():
             y_send(i).start()
-
-    stage_a(0, True)
 
     def outer(k, carry):
         def upto(k):
             return (1 - chip) * (2 + k // 2 + k // 3) + chip * (3 + (k + 2) // 3)
 
         def one(t, c):
-            stage_a(t, False)
+            stage_a(t)
             return c
 
-        low = jnp.where(k == 0, 1, upto(k - 1)) if not isinstance(k, int) else (1 if k == 0 else upto(k - 1))
-        lax.fori_loop(low, upto(k), one, 0)
-        for i in range(n):
-            pl.when(k == i)(functools.partial(stage_b, i))
+        lax.fori_loop(jnp.where(k == 0, 0, upto(k - 1)), upto(k), one, 0)
+        stage_b(k)
         return carry
 
     lax.fori_loop(0, n, outer, 0)
@@ -196,8 +233,8 @@
     row_spec = P("data", "seq", None)
 
     def local_block(act_in, ln1_scale, ln1_bias, w_in, b_in, ln2_scale, ln2_bias, w_spatial, b_spatial, causal_mask, w_out, b_out):
-        batch, rows, width = act_in.shape
-        length = batch * 0 + n * rows
+        rows, width = act_in.shape[1:]
+        length = n * rows
         gate = w_out.shape[0]
         hbm = pl.BlockSpec(memory_space=pl.ANY)
         vmem = pl.BlockSpec(memory_space=pltpu.VMEM)
@@ -216,12 +253,13 @@
                 pltpu.VMEM((gate, width), BF16),
                 pltpu.VMEM((length, length), BF16),
                 pltpu.VMEM((length, length), jnp.int32),
-                pltpu.VMEM((length, gate), BF16),
-                pltpu.VMEM((length, gate), BF16),
+                pltpu.VMEM((length, 2 * gate), BF16),
                 pltpu.VMEM((rows, width), BF16),
                 pltpu.VMEM((rows, gate), BF16),
                 pltpu.VMEM((n, rows, width), BF16),
-                pltpu.VMEM((length, 128), F32),
+                pltpu.VMEM((rows, 128), F32),
+                pltpu.VMEM((rows, COLS), F32),
+                pltpu.VMEM((rows, COLS), F32),
                 pltpu.SemaphoreType.DMA((n,)),
                 pltpu.SemaphoreType.DMA((n,)),
                 pltpu.SemaphoreType.DMA((n,)),

time: 70.8 us -> 80.5 us (1.14)
  Pallas kernels: 67.5 us -> 77.2 us
    pallas_call x1, Pallas kernels: 67.5 us -> 77.2 us  [local_block(): pl.pallas_call(functools.partial(body, n), out_shape=jax.ShapeDtypeStruct...]
where the time goes in v2:
time: 80.5 us; the launch traced here: 80.3 us
  Pallas kernels  77.2 us (96%)
  local copies, waits for them, and re-layouts  3.08 us (4%)
    pallas_call x1, Pallas kernels, local_block(): pl.pallas_call(functools.partial(body, n), out_shape=jax.ShapeDtypeStruct...  77.2 us
    unnamed x1, local copies, waits for them, and re-layouts  3.08 us

profile of v2, /device:TPU:0, one launch (start us, length us, event | category | flops | bytes accessed | tf_op | source)
XLA Modules:
  0.0 80.3 jit_solution(16355724552194455214)
XLA Ops:
  0.0 77.2 %gmlp.1 = bf16[4,256,1024]{2,1,0:T(8,128)(2,1)} custom-call(bf16[4,256,1024]{2,1,0:T(8,128)(2,1)} %act.1, f32[1,1024]{1,0:T(1,128)} %bitcast.10, f32[1,1024]{1,0:T(1,128)} %bitcast.11, bf16[1024,6144]{1,0:T(8,128)(2,1)} %w_in.1, f32[1,6144]{1,0:T(1,128)} %bitcast.7, f32[1,3072]{1,0:T(1,128)} %bitcast.8, f32[1,3072]{1,0:T(1,128)} %bitcast.9, ...), custom_call_target="tpu_custom_call" | custom-call | tf_op jit(solution)/shard_map/gmlp/pallas_call | solution.py:245
  77.2 3.1 %copy.14 = bf16[4,256,1024]{2,1,0:T(8,128)(2,1)} copy(bf16[4,256,1024]{2,1,0:T(8,128)(2,1)} %gmlp.1) | data formatting | bytes 4194304

commit v3 on v1

--- a/solution.py
+++ b/solution.py
@@ -124,18 +124,19 @@
             acc = jnp.dot(u[...], wi[:, cols], preferred_element_type=F32)
             return gelu(acc + b_in[:, cols]).astype(BF16)
 
+        step2 = 16
+        tiles = rows // step2
+
+        def norm(r):
+            part = pl.ds(at + r * step2, step2)
+            vn[part, :] = layer_norm(vn[part, :].astype(F32), ln2s[...], ln2b[...]).astype(BF16)
+
         for c in range(n_cols):
             vn[pl.ds(at, rows), pl.ds(c * COLS, COLS)] = chunk(n_cols + c)
         for c in range(n_cols):
             g[pl.ds(at, rows), pl.ds(c * COLS, COLS)] = chunk(c)
-        step2 = 16
-
-        def norm(r, carry):
-            part = pl.ds(pl.multiple_of(at + r * step2, step2), step2)
-            vn[part, :] = layer_norm(vn[part, :].astype(F32), ln2s[...], ln2b[...]).astype(BF16)
-            return carry
-
-        lax.fori_loop(0, rows // step2, norm, 0)
+            for r in range(c * tiles // n_cols, (c + 1) * tiles // n_cols):
+                norm(r)
 
     def stage_b(i):
         at = pl.ds(i * rows, rows)
@@ -196,8 +197,8 @@
     row_spec = P("data", "seq", None)
 
     def local_block(act_in, ln1_scale, ln1_bias, w_in, b_in, ln2_scale, ln2_bias, w_spatial, b_spatial, causal_mask, w_out, b_out):
-        batch, rows, width = act_in.shape
-        length = batch * 0 + n * rows
+        rows, width = act_in.shape[1:]
+        length = n * rows
         gate = w_out.shape[0]
         hbm = pl.BlockSpec(memory_space=pl.ANY)
         vmem = pl.BlockSpec(memory_space=pltpu.VMEM)

time: 70.8 us -> 61.2 us (0.86)
  the two profiles are of different devices: /device:TPU:0 before, /device:TPU:7 now
where the time goes in v3:
time: 61.2 us; the launch traced here: 61 us
  Pallas kernels  57.9 us (95%)
  local copies, waits for them, and re-layouts  3.08 us (5%)
    pallas_call x1, Pallas kernels, local_block(): pl.pallas_call(functools.partial(body, n), out_shape=jax.ShapeDtypeStruct...  57.9 us
    unnamed x1, local copies, waits for them, and re-layouts  3.08 us

profile of v3, /device:TPU:7, one launch (start us, length us, event | category | flops | bytes accessed | tf_op | source)
XLA Modules:
  0.0 61.0 jit_solution(10324174966006910521)
XLA Ops:
  0.0 57.9 %gmlp.1 = bf16[4,256,1024]{2,1,0:T(8,128)(2,1)} custom-call(bf16[4,256,1024]{2,1,0:T(8,128)(2,1)} %act.1, f32[1,1024]{1,0:T(1,128)} %bitcast.10, f32[1,1024]{1,0:T(1,128)} %bitcast.11, bf16[1024,6144]{1,0:T(8,128)(2,1)} %w_in.1, f32[1,6144]{1,0:T(1,128)} %bitcast.7, f32[1,3072]{1,0:T(1,128)} %bitcast.8, f32[1,3072]{1,0:T(1,128)} %bitcast.9, ...), custom_call_target="tpu_custom_call" | custom-call | tf_op jit(solution)/shard_map/gmlp/pallas_call | solution.py:209
  57.9 3.1 %copy.14 = bf16[4,256,1024]{2,1,0:T(8,128)(2,1)} copy(bf16[4,256,1024]{2,1,0:T(8,128)(2,1)} %gmlp.1) | data formatting | bytes 4194304

commit v4 on v3

v4 whole, which is shorter than its diff:
```python
import functools

import jax
import jax.numpy as jnp
from jax import lax
from jax.experimental import pallas as pl
from jax.experimental.pallas import tpu as pltpu
from jax.sharding import PartitionSpec as P

LN_EPS = 1e-6
GELU_A = 0.7978845608028654
GELU_B = GELU_A * 0.044715
COLS = 512
MESH = pl.DeviceIdType.MESH
F32 = jnp.float32
BF16 = jnp.bfloat16


def gelu(a):
    return a * jax.nn.sigmoid(a * (2 * GELU_A + 2 * GELU_B * (a * a)))


def layer_norm(x, gain, shift):
    width = x.shape[-1]
    mean = jnp.sum(x, axis=-1, keepdims=True) * (1.0 / width)
    centered = x - mean
    var = jnp.sum(centered * centered, axis=-1, keepdims=True) * (1.0 / width)
    return centered * lax.rsqrt(var + LN_EPS) * gain + shift


def body(n, act, ln1s, ln1b, w_in, b_in, ln2s, ln2b, w_sp, b_sp, mask, w_out, b_out, out,
         xbuf, wi, wo, ws, mk, vn, g, u, q, ybuf, bias, stat,
         xs_sem, xr_sem, ys_sem, yr_sem, wi_sem, wo_sem, ws_sem, mk_sem):
    me = lax.axis_index("seq")
    chip, core = me // 2, lax.rem(me, 2)
    partner = chip * 2 + 1 - core
    far = (1 - chip) * 2
    rows, width = act.shape[1], act.shape[2]
    half = rows // 2
    gate = w_out.shape[0]
    n_cols = gate // COLS

    def wi_copy(c):
        cols = pl.ds(c * COLS, COLS)
        return pltpu.make_async_copy(w_in.at[:, cols], wi.at[:, cols], wi_sem.at[c])

    def ws_copy(i):
        where = (pl.ds(i * rows, rows), pl.ds(0, (i + 1) * rows))
        return pltpu.make_async_copy(w_sp.at[where], ws.at[where], ws_sem.at[i])

    def mk_copy(i):
        where = (pl.ds(i * rows, rows), pl.ds(0, (i + 1) * rows))
        return pltpu.make_async_copy(mask.at[where], mk.at[where], mk_sem.at[i])

    def wo_copy():
        return pltpu.make_async_copy(w_out, wo, wo_sem)

    def own_x(p):
        part = pl.ds(p * half, half)
        return pltpu.make_async_copy(act.at[me, part], xbuf.at[me, part], xr_sem.at[me, p])

    def x_send(dest, p):
        part = pl.ds(p * half, half)
        return pltpu.make_async_remote_copy(
            src_ref=act.at[dest, part], dst_ref=xbuf.at[me, part], send_sem=xs_sem.at[dest, p], recv_sem=xr_sem.at[me, p],
            device_id={"seq": dest}, device_id_type=MESH)

    def x_recv(block, p):
        part = pl.ds(p * half, half)
        return pltpu.make_async_remote_copy(
            src_ref=act.at[block, part], dst_ref=xbuf.at[block, part], send_sem=xs_sem.at[block, p],
            recv_sem=xr_sem.at[block, p], device_id={"seq": block}, device_id_type=MESH)

    def y_send(block, c):
        cols = pl.ds(c * COLS, COLS)
        return pltpu.make_async_remote_copy(
            src_ref=ybuf.at[block, :, cols], dst_ref=out.at[me, :, cols], send_sem=ys_sem.at[block, c],
            recv_sem=yr_sem.at[me, c], device_id={"seq": block}, device_id_type=MESH)

    def y_recv(block, c):
        cols = pl.ds(c * COLS, COLS)
        return pltpu.make_async_remote_copy(
            src_ref=ybuf.at[block, :, cols], dst_ref=out.at[block, :, cols], send_sem=ys_sem.at[block, c],
            recv_sem=yr_sem.at[block, c], device_id={"seq": block}, device_id_type=MESH)

    def y_own(c):
        cols = pl.ds(c * COLS, COLS)
        return pltpu.make_async_copy(ybuf.at[me, :, cols], out.at[me, :, cols], yr_sem.at[me, c])

    barrier = pltpu.get_barrier_semaphore()
    for k in range(1, n):
        pl.semaphore_signal(barrier, inc=1, device_id={"seq": lax.rem(me + k, n)}, device_id_type=MESH)
    for p in range(2):
        own_x(p).start()
    order = list(range(n_cols, 2 * n_cols)) + list(range(n_cols))
    for c in order:
        wi_copy(c).start()
    pl.semaphore_wait(barrier, n - 1)
    for dest in (far, partner, far + 1):
        for p in range(2):
            x_send(dest, p).start()
    for i in range(n):
        ws_copy(i).start()
        mk_copy(i).start()
    wo_copy().start()

    for i in range(n):
        at = pl.ds(i * rows, rows)
        bias[at, :] = jnp.broadcast_to(b_sp[:, at], (128, rows)).T

    def stage_a(t, first):
        if first:
            pieces = [(me, 0), (me, 1)]
            for p in range(2):
                own_x(p).wait()
        else:
            remote = t // 2
            side = t - 2
            pieces = [((1 - remote) * partner + remote * far, remote * side),
                      ((1 - remote) * partner + remote * (far + 1), (1 - remote) + remote * side)]
            for block, p in pieces:
                x_recv(block, p).wait_recv()
        starts = [pl.multiple_of(block * rows + p * half, half) for block, p in pieces]
        step1 = 64
        for k, (block, p) in enumerate(pieces):
            for r in range(half // step1):
                x = xbuf[block, pl.ds(pl.multiple_of(p * half, half) + r * step1, step1), :].astype(F32)
                u[pl.ds(k * half + r * step1, step1), :] = layer_norm(x, ln1s[...], ln1b[...]).astype(BF16)

        def chunk(c, dst, dst_c):
            if first:
                wi_copy(c).wait()
            cols = pl.ds(c * COLS, COLS)
            acc = jnp.dot(u[...], wi[:, cols], preferred_element_type=F32)
            value = gelu(acc + b_in[:, cols]).astype(BF16)
            for k in range(2):
                dst[pl.ds(starts[k], half), pl.ds(dst_c * COLS, COLS)] = value[k * half:(k + 1) * half]
            return value

        lanes = 128
        per_lane = gate // lanes
        for c in range(n_cols):
            value = chunk(n_cols + c, vn, c).astype(F32)
            tiles = [value[:, j * lanes:(j + 1) * lanes] for j in range(COLS // lanes)]
            if c == 0:
                pivot = tiles[0]
                stat[0] = pivot
                tiles = tiles[1:]
            else:
                pivot = stat[0]
            diffs = [v - pivot for v in tiles]
            total = sum(diffs[1:], diffs[0])
            squares = sum([d * d for d in diffs[1:]], diffs[0] * diffs[0])
            stat[1] = total if c == 0 else stat[1] + total
            stat[2] = squares if c == 0 else stat[2] + squares
        total = stat[1]
        mean_lane = stat[0] + total * (1.0 / per_lane)
        mean = jnp.sum(mean_lane, axis=-1, keepdims=True) * (1.0 / lanes)
        away = mean_lane - mean
        spread = (stat[2] - total * total * (1.0 / per_lane)) + per_lane * (away * away)
        var = jnp.maximum(jnp.sum(spread, axis=-1, keepdims=True) * (1.0 / gate), 0.0)
        stat[0] = jnp.broadcast_to(mean, (rows, lanes))
        stat[1] = jnp.broadcast_to(lax.rsqrt(var + LN_EPS), (rows, lanes))
        step2 = 16
        tiles = rows // step2

        def norm(r):
            part = pl.ds(starts[r * step2 // half] + r * step2 % half, step2)
            here = pl.ds(r * step2, step2)
            mean = jnp.concatenate([stat[0, here]] * per_lane, axis=1)
            scale = jnp.concatenate([stat[1, here]] * per_lane, axis=1)
            vn[part, :] = ((vn[part, :].astype(F32) - mean) * scale * ln2s[...] + ln2b[...]).astype(BF16)

        for c in range(n_cols):
            chunk(c, g, c)
            for r in range(c * tiles // n_cols, (c + 1) * tiles // n_cols):
                norm(r)

    def stage_b(i):
        at = pl.ds(i * rows, rows)
        depth = (i + 1) * rows
        ws_copy(i).wait()
        mk_copy(i).wait()
        for r in range(i + 1):
            cols = pl.ds(r * rows, rows)
            ws[at, cols] = jnp.where(mk[at, cols] > 0, ws[at, cols].astype(F32), 0.0).astype(BF16)
        bias_cols = jnp.concatenate([bias[at, :]] * (COLS // 128), axis=1)
        for c in range(n_cols):
            cols = pl.ds(c * COLS, COLS)
            s = jnp.dot(ws[at, :depth], vn[:depth, cols], preferred_element_type=F32) + bias_cols
            q[:, cols] = (g[at, cols].astype(F32) * s.astype(BF16).astype(F32)).astype(BF16)
        for c in range(width // COLS):
            cols = pl.ds(c * COLS, COLS)
            y = jnp.dot(q[...], wo[:, cols], preferred_element_type=F32) + b_out[:, cols]
            ybuf[i, :, cols] = (xbuf[i, :, cols].astype(F32) + y).astype(BF16)

            @pl.when(me == i)
            def _():
                y_own(c).start()

            @pl.when(me != i)
            def _():
                y_send(i, c).start()

    stage_a(0, True)
    even0 = (1 - chip) * (1 - core)
    odd0 = (1 - chip) * core

    def outer(k, carry):
        def upto(k):
            return n - 2 * odd0 * (1 - k // 2)

        def one(t, c):
            stage_a(t, False)
            return c

        lax.fori_loop(jnp.where(k == 0, 1, upto(k - 1)), upto(k), one, 0)

        @pl.when(k == 0)
        def _():
            wo_copy().wait()

        block = lax.rem(k + 2 * even0, n)
        for i in range(n):
            pl.when(block == i)(functools.partial(stage_b, i))
        return carry

    lax.fori_loop(0, n, outer, 0)

    for k in range(1, n):
        peer = lax.rem(me + k, n)
        for p in range(2):
            x_send(peer, p).wait_send()
            y_send(peer, p).wait_send()
            y_recv(peer, p).wait_recv()
    for p in range(2):
        y_own(p).wait()


def solution(mesh):
    n = mesh.shape["seq"]
    row_spec = P("data", "seq", None)

    def local_block(act_in, ln1_scale, ln1_bias, w_in, b_in, ln2_scale, ln2_bias, w_spatial, b_spatial, causal_mask, w_out, b_out):
        rows, width = act_in.shape[1:]
        length = n * rows
        gate = w_out.shape[0]
        hbm = pl.BlockSpec(memory_space=pl.ANY)
        vmem = pl.BlockSpec(memory_space=pltpu.VMEM)

        def row(v):
            return v.reshape(1, -1)

        return pl.pallas_call(
            functools.partial(body, n),
            out_shape=jax.ShapeDtypeStruct(act_in.shape, act_in.dtype),
            in_specs=[hbm, vmem, vmem, hbm, vmem, vmem, vmem, hbm, vmem, hbm, hbm, vmem],
            out_specs=hbm,
            scratch_shapes=[
                pltpu.VMEM((n, rows, width), BF16),
                pltpu.VMEM((width, 2 * gate), BF16),
                pltpu.VMEM((gate, width), BF16),
                pltpu.VMEM((length, length), BF16),
                pltpu.VMEM((length, length), jnp.int32),
                pltpu.VMEM((length, gate), BF16),
                pltpu.VMEM((length, gate), BF16),
                pltpu.VMEM((rows, width), BF16),
                pltpu.VMEM((rows, gate), BF16),
                pltpu.VMEM((n, rows, width), BF16),
                pltpu.VMEM((length, 128), F32),
                pltpu.VMEM((3, rows, 128), F32),
                pltpu.SemaphoreType.DMA((n, 2)),
                pltpu.SemaphoreType.DMA((n, 2)),
                pltpu.SemaphoreType.DMA((n, width // COLS)),
                pltpu.SemaphoreType.DMA((n, width // COLS)),
                pltpu.SemaphoreType.DMA((2 * gate // COLS,)),
                pltpu.SemaphoreType.DMA,
                pltpu.SemaphoreType.DMA((n,)),
                pltpu.SemaphoreType.DMA((n,)),
            ],
            compiler_params=pltpu.CompilerParams(
                collective_id=0, has_side_effects=True, vmem_limit_bytes=60 * 1024 * 1024),
            name="gmlp",
        )(act_in, row(ln1_scale), row(ln1_bias), w_in, row(b_in), row(ln2_scale), row(ln2_bias),
          w_spatial, row(b_spatial), causal_mask, w_out, row(b_out))

    return jax.shard_map(local_block, mesh=mesh, in_specs=(row_spec,) + (P(),) * 11, out_specs=row_spec, check_vma=False)
```

time: 61.2 us -> 63.3 us (1.034)
  the two profiles are of different devices: /device:TPU:7 before, /device:TPU:1 now
where the time goes in v4:
time: 63.3 us; the launch traced here: 63.1 us
  Pallas kernels  60 us (95%)
  local copies, waits for them, and re-layouts  3.08 us (5%)
    pallas_call x1, Pallas kernels, local_block(): pl.pallas_call(functools.partial(body, n), out_shape=jax.ShapeDtypeStruct...  60 us
    unnamed x1, local copies, waits for them, and re-layouts  3.08 us

profile of v4, /device:TPU:1, one launch (start us, length us, event | category | flops | bytes accessed | tf_op | source)
XLA Modules:
  0.0 63.1 jit_solution(15789006063936089908)
XLA Ops:
  0.0 60.0 %gmlp.1 = bf16[4,256,1024]{2,1,0:T(8,128)(2,1)} custom-call(bf16[4,256,1024]{2,1,0:T(8,128)(2,1)} %act.1, f32[1,1024]{1,0:T(1,128)} %bitcast.10, f32[1,1024]{1,0:T(1,128)} %bitcast.11, bf16[1024,6144]{1,0:T(8,128)(2,1)} %w_in.1, f32[1,6144]{1,0:T(1,128)} %bitcast.7, f32[1,3072]{1,0:T(1,128)} %bitcast.8, f32[1,3072]{1,0:T(1,128)} %bitcast.9, ...), custom_call_target="tpu_custom_call" | custom-call | tf_op jit(solution)/shard_map/gmlp/pallas_call | solution.py:254
  60.0 3.1 %copy.14 = bf16[4,256,1024]{2,1,0:T(8,128)(2,1)} copy(bf16[4,256,1024]{2,1,0:T(8,128)(2,1)} %gmlp.1) | data formatting | bytes 4194304

commit v5 on v4

v5 whole, which is shorter than its diff:
```python
import functools

import jax
import jax.numpy as jnp
from jax import lax
from jax.experimental import pallas as pl
from jax.experimental.pallas import tpu as pltpu
from jax.sharding import PartitionSpec as P

LN_EPS = 1e-6
GELU_A = 0.7978845608028654
GELU_B = GELU_A * 0.044715
COLS = 512
LANES = 128
MESH = pl.DeviceIdType.MESH
F32 = jnp.float32
BF16 = jnp.bfloat16


def gelu(a):
    return a * jax.nn.sigmoid(a * (2 * GELU_A + 2 * GELU_B * (a * a)))


def layer_norm(x, gain, shift):
    width = x.shape[-1]
    mean = jnp.sum(x, axis=-1, keepdims=True) * (1.0 / width)
    centered = x - mean
    var = jnp.sum(centered * centered, axis=-1, keepdims=True) * (1.0 / width)
    return centered * lax.rsqrt(var + LN_EPS) * gain + shift


def wide(ref, tiles, *where):
    return jnp.concatenate([ref[(j, *where)] for j in tiles], axis=1)


def body(n, act, ln1s, ln1b, w_in, b_in, ln2s, ln2b, w_sp, b_sp, mask, w_out, b_out, out,
         xbuf, wi, wo, ws, mk, vn, g, u, q, ybuf, bias, stat,
         xs_sem, xr_sem, ys_sem, yr_sem, wi_sem, wo_sem, ws_sem, mk_sem):
    me = lax.axis_index("seq")
    chip, core = me // 2, lax.rem(me, 2)
    partner = chip * 2 + 1 - core
    far = (1 - chip) * 2
    rows, width = act.shape[1], act.shape[2]
    length = n * rows
    half = rows // 2
    gate = w_out.shape[0]
    gate_tiles = gate // LANES
    n_cols = gate // COLS
    per = COLS // LANES

    def lanes(j):
        return pl.ds(j * LANES, LANES)

    def wi_copy(j):
        return pltpu.make_async_copy(w_in.at[:, lanes(j)], wi.at[j], wi_sem.at[j])

    def ws_copy(j):
        return pltpu.make_async_copy(w_sp.at[:, lanes(j)], ws.at[j], ws_sem.at[j])

    def wo_copy(j):
        return pltpu.make_async_copy(w_out.at[:, lanes(j)], wo.at[j], wo_sem.at[j])

    def mk_copy():
        return pltpu.make_async_copy(mask, mk, mk_sem)

    def own_x(p):
        part = pl.ds(p * half, half)
        return pltpu.make_async_copy(act.at[me, part], xbuf.at[me, part], xr_sem.at[me, p])

    def x_send(dest, p):
        part = pl.ds(p * half, half)
        return pltpu.make_async_remote_copy(
            src_ref=act.at[dest, part], dst_ref=xbuf.at[me, part], send_sem=xs_sem.at[dest, p], recv_sem=xr_sem.at[me, p],
            device_id={"seq": dest}, device_id_type=MESH)

    def x_recv(block, p):
        part = pl.ds(p * half, half)
        return pltpu.make_async_remote_copy(
            src_ref=act.at[block, part], dst_ref=xbuf.at[block, part], send_sem=xs_sem.at[block, p],
            recv_sem=xr_sem.at[block, p], device_id={"seq": block}, device_id_type=MESH)

    def y_send(block):
        return pltpu.make_async_remote_copy(
            src_ref=ybuf.at[block], dst_ref=out.at[me], send_sem=ys_sem.at[block], recv_sem=yr_sem.at[me],
            device_id={"seq": block}, device_id_type=MESH)

    def y_recv(block):
        return pltpu.make_async_remote_copy(
            src_ref=ybuf.at[block], dst_ref=out.at[block], send_sem=ys_sem.at[block], recv_sem=yr_sem.at[block],
            device_id={"seq": block}, device_id_type=MESH)

    def y_own():
        return pltpu.make_async_copy(ybuf.at[me], out.at[me], yr_sem.at[me])

    barrier = pltpu.get_barrier_semaphore()
    for k in range(1, n):
        pl.semaphore_signal(barrier, inc=1, device_id={"seq": lax.rem(me + k, n)}, device_id_type=MESH)
    for p in range(2):
        own_x(p).start()
    for j in range(2 * gate_tiles):
        wi_copy((j + gate_tiles) % (2 * gate_tiles)).start()
    pl.semaphore_wait(barrier, n - 1)
    for dest in (far, partner, far + 1):
        for p in range(2):
            x_send(dest, p).start()
    for j in range(length // LANES):
        ws_copy(j).start()
    mk_copy().start()
    for j in range(width // LANES):
        wo_copy(j).start()

    for i in range(n):
        at = pl.ds(i * rows, rows)
        bias[at, :] = jnp.broadcast_to(b_sp[:, at], (LANES, rows)).T

    def stage_a(t, first):
        if first:
            pieces = [(me, 0), (me, 1)]
            for p in range(2):
                own_x(p).wait()
        else:
            remote = t // 2
            side = t - 2
            pieces = [((1 - remote) * partner + remote * far, remote * side),
                      ((1 - remote) * partner + remote * (far + 1), (1 - remote) + remote * side)]
            for block, p in pieces:
                x_recv(block, p).wait_recv()
        starts = [pl.multiple_of(block * rows + p * half, half) for block, p in pieces]
        step1 = 64
        for k, (block, p) in enumerate(pieces):
            for r in range(half // step1):
                x = xbuf[block, pl.ds(pl.multiple_of(p * half, half) + r * step1, step1), :].astype(F32)
                x = layer_norm(x, ln1s[...], ln1b[...]).astype(BF16)
                for j in range(width // LANES):
                    u[j, pl.ds(k * half + r * step1, step1), :] = x[:, j * LANES:(j + 1) * LANES]

        def chunk(c):
            tiles = range(c * per, (c + 1) * per)
            acc = jnp.dot(wide(u, range(width // LANES)), wide(wi, tiles), preferred_element_type=F32)
            return gelu(acc + b_in[:, pl.ds(c * COLS, COLS)]).astype(BF16)

        def put(dst, c, value):
            for j in range(per):
                for k in range(2):
                    dst[c * per + j, pl.ds(starts[k], half), :] = value[k * half:(k + 1) * half, j * LANES:(j + 1) * LANES]

        if first:
            for j in range(gate_tiles, 2 * gate_tiles):
                wi_copy(j).wait()
        for c in range(n_cols):
            value = chunk(n_cols + c)
            put(vn, c, value)
            value = value.astype(F32)
            tiles = [value[:, j * LANES:(j + 1) * LANES] for j in range(per)]
            if c == 0:
                pivot = tiles[0]
                stat[0] = pivot
                tiles = tiles[1:]
            else:
                pivot = stat[0]
            diffs = [v - pivot for v in tiles]
            total = sum(diffs[1:], diffs[0])
            squares = sum([d * d for d in diffs[1:]], diffs[0] * diffs[0])
            stat[1] = total if c == 0 else stat[1] + total
            stat[2] = squares if c == 0 else stat[2] + squares
        if first:
            for j in range(gate_tiles):
                wi_copy(j).wait()
        total = stat[1]
        mean_lane = stat[0] + total * (1.0 / gate_tiles)
        mean = jnp.sum(mean_lane, axis=-1, keepdims=True) * (1.0 / LANES)
        away = mean_lane - mean
        spread = (stat[2] - total * total * (1.0 / gate_tiles)) + gate_tiles * (away * away)
        var = jnp.maximum(jnp.sum(spread, axis=-1, keepdims=True) * (1.0 / gate), 0.0)
        stat[0] = jnp.broadcast_to(mean, (rows, LANES))
        stat[1] = jnp.broadcast_to(lax.rsqrt(var + LN_EPS), (rows, LANES))

        def norm(j):
            for k in range(2):
                part = pl.ds(starts[k], half)
                here = pl.ds(k * half, half)
                value = (vn[j, part, :].astype(F32) - stat[0, here]) * stat[1, here]
                vn[j, part, :] = (value * ln2s[:, lanes(j)] + ln2b[:, lanes(j)]).astype(BF16)

        for c in range(n_cols):
            put(g, c, chunk(c))
            for j in range(c * per, (c + 1) * per):
                norm(j)

    def stage_b(i):
        at = pl.ds(i * rows, rows)
        depth = (i + 1) * rows
        for j in range(depth // LANES):
            ws[j, at, :] = jnp.where(mk[at, lanes(j)] > 0, ws[j, at, :].astype(F32), 0.0).astype(BF16)
        for c in range(n_cols):
            tiles = range(c * per, (c + 1) * per)
            s = jnp.dot(wide(ws, range(depth // LANES), at), wide(vn, tiles, pl.ds(0, depth)), preferred_element_type=F32)
            for j in range(per):
                t = (s[:, j * LANES:(j + 1) * LANES] + bias[at, :]).astype(BF16).astype(F32)
                q[tiles[j]] = (g[tiles[j], at, :].astype(F32) * t).astype(BF16)
        for c in range(width // COLS):
            cols = pl.ds(c * COLS, COLS)
            y = jnp.dot(wide(q, range(gate_tiles)), wide(wo, range(c * per, (c + 1) * per)), preferred_element_type=F32)
            ybuf[i, :, cols] = (xbuf[i, :, cols].astype(F32) + (y + b_out[:, cols])).astype(BF16)

    stage_a(0, True)
    even0 = (1 - chip) * (1 - core)
    odd0 = (1 - chip) * core

    def outer(k, carry):
        def upto(k):
            return n - 2 * odd0 * (1 - k // 2)

        def one(t, c):
            stage_a(t, False)
            return c

        lax.fori_loop(jnp.where(k == 0, 1, upto(k - 1)), upto(k), one, 0)

        @pl.when(k == 0)
        def _():
            for j in range(length // LANES):
                ws_copy(j).wait()
            mk_copy().wait()
            for j in range(width // LANES):
                wo_copy(j).wait()

        block = lax.rem(k + 2 * even0, n)
        for i in range(n):
            pl.when(block == i)(functools.partial(stage_b, i))

        @pl.when(me == block)
        def _():
            y_own().start()

        @pl.when(me != block)
        def _():
            y_send(block).start()

        return carry

    lax.fori_loop(0, n, outer, 0)

    for k in range(1, n):
        peer = lax.rem(me + k, n)
        for p in range(2):
            x_send(peer, p).wait_send()
        y_send(peer).wait_send()
        y_recv(peer).wait_recv()
    y_own().wait()


def solution(mesh):
    n = mesh.shape["seq"]
    row_spec = P("data", "seq", None)

    def local_block(act_in, ln1_scale, ln1_bias, w_in, b_in, ln2_scale, ln2_bias, w_spatial, b_spatial, causal_mask, w_out, b_out):
        rows, width = act_in.shape[1:]
        length = n * rows
        gate = w_out.shape[0]
        hbm = pl.BlockSpec(memory_space=pl.ANY)
        vmem = pl.BlockSpec(memory_space=pltpu.VMEM)

        def row(v):
            return v.reshape(1, -1)

        return pl.pallas_call(
            functools.partial(body, n),
            out_shape=jax.ShapeDtypeStruct(act_in.shape, act_in.dtype),
            in_specs=[hbm, vmem, vmem, hbm, vmem, vmem, vmem, hbm, vmem, hbm, hbm, vmem],
            out_specs=hbm,
            scratch_shapes=[
                pltpu.VMEM((n, rows, width), BF16),
                pltpu.VMEM((2 * gate // LANES, width, LANES), BF16),
                pltpu.VMEM((width // LANES, gate, LANES), BF16),
                pltpu.VMEM((length // LANES, length, LANES), BF16),
                pltpu.VMEM((length, length), jnp.int32),
                pltpu.VMEM((gate // LANES, length, LANES), BF16),
                pltpu.VMEM((gate // LANES, length, LANES), BF16),
                pltpu.VMEM((width // LANES, rows, LANES), BF16),
                pltpu.VMEM((gate // LANES, rows, LANES), BF16),
                pltpu.VMEM((n, rows, width), BF16),
                pltpu.VMEM((length, LANES), F32),
                pltpu.VMEM((3, rows, LANES), F32),
                pltpu.SemaphoreType.DMA((n, 2)),
                pltpu.SemaphoreType.DMA((n, 2)),
                pltpu.SemaphoreType.DMA((n,)),
                pltpu.SemaphoreType.DMA((n,)),
                pltpu.SemaphoreType.DMA((2 * gate // LANES,)),
                pltpu.SemaphoreType.DMA((width // LANES,)),
                pltpu.SemaphoreType.DMA((length // LANES,)),
                pltpu.SemaphoreType.DMA,
            ],
            compiler_params=pltpu.CompilerParams(
                collective_id=0, has_side_effects=True, vmem_limit_bytes=60 * 1024 * 1024),
            name="gmlp",
        )(act_in, row(ln1_scale), row(ln1_bias), w_in, row(b_in), row(ln2_scale), row(ln2_bias),
          w_spatial, row(b_spatial), causal_mask, w_out, row(b_out))

    return jax.shard_map(local_block, mesh=mesh, in_specs=(row_spec,) + (P(),) * 11, out_specs=row_spec, check_vma=False)
```

time: 63.3 us -> 60.4 us (0.954)
  Pallas kernels: 60 us -> 57.1 us
    pallas_call x1, Pallas kernels: 60 us -> 57.1 us  [local_block(): pl.pallas_call(functools.partial(body, n), out_shape=jax.ShapeDtypeStruct...]
where the time goes in v5:
time: 60.4 us; the launch traced here: 60.2 us
  Pallas kernels  57.1 us (95%)
  local copies, waits for them, and re-layouts  3.08 us (5%)
    pallas_call x1, Pallas kernels, local_block(): pl.pallas_call(functools.partial(body, n), out_shape=jax.ShapeDtypeStruct...  57.1 us
    unnamed x1, local copies, waits for them, and re-layouts  3.08 us

profile of v5, /device:TPU:1, one launch (start us, length us, event | category | flops | bytes accessed | tf_op | source)
XLA Modules:
  0.0 60.2 jit_solution(6344438495159911595)
XLA Ops:
  0.0 57.1 %gmlp.1 = bf16[4,256,1024]{2,1,0:T(8,128)(2,1)} custom-call(bf16[4,256,1024]{2,1,0:T(8,128)(2,1)} %act.1, f32[1,1024]{1,0:T(1,128)} %bitcast.10, f32[1,1024]{1,0:T(1,128)} %bitcast.11, bf16[1024,6144]{1,0:T(8,128)(2,1)} %w_in.1, f32[1,6144]{1,0:T(1,128)} %bitcast.7, f32[1,3072]{1,0:T(1,128)} %bitcast.8, f32[1,3072]{1,0:T(1,128)} %bitcast.9, ...), custom_call_target="tpu_custom_call" | custom-call | tf_op jit(solution)/shard_map/gmlp/pallas_call | solution.py:267
  57.1 3.1 %copy.14 = bf16[4,256,1024]{2,1,0:T(8,128)(2,1)} copy(bf16[4,256,1024]{2,1,0:T(8,128)(2,1)} %gmlp.1) | data formatting | bytes 4194304
